TPU v7x, 32 devices: a whole 2x2x4 slice. The times are simulated.
32 devices in a mesh: dp: 4 (over x, core), mp: 8 (over z, y).
Axes of the slice: x: 2, y: 2, z: 4, core: 2. Of those that a mesh axis runs over, the one named last changes fastest.
Arguments:
- cotangent: bfloat16 [512, 4608], P(('dp', 'mp')), may hold values from -50 to 50
- mlp_out: bfloat16 [512, 4608], P(('dp', 'mp')), may hold values from -500 to 500
- post_gain: float32 [4608], replicated, may hold values from 0.5 to 1.5
- down_weight: bfloat16 [36864, 4608], P('mp', 'dp'), may hold values from -0.09375 to 0.09375
- gate_pre: bfloat16 [512, 36864], P('dp', 'mp'), may hold values from -6 to 6
- up_pre: bfloat16 [512, 36864], P('dp', 'mp'), may hold values from -6 to 6
Outputs:
- gate_grad: float32 [512, 36864], P('dp', 'mp')
- up_grad: float32 [512, 36864], P('dp', 'mp')
- gain_grad: float32 [4608], replicated
All inputs are finite; a program needn't handle non-finite values.
Results may differ from a plain program's by a relative error of at most 0.0005.
Values may be sent and summed in bfloat16 or wider, within the bound.
A program may use at most 64 MiB of HBM per device.

v0:
```python
import jax
import jax.numpy as jnp
from jax import lax
from jax.sharding import PartitionSpec as P

D = 4608


epsilon = 1e-06


def gelu_tanh(values):
    return jax.nn.gelu(values, approximate=True)


def local(cotangent, mlp_out, post_gain, down_weight, gate_pre, up_pre):
    forward = mlp_out.astype(jnp.float32)
    upstream = cotangent.astype(jnp.float32)
    root_mean = jnp.sqrt(jnp.mean(forward * forward, axis=1, keepdims=True) + epsilon)
    normed = forward / root_mean
    gain_part = jnp.sum(upstream * normed, axis=0)
    scaled = upstream * post_gain[None, :]
    project_sum = jnp.sum(scaled * forward, axis=1, keepdims=True)
    out_grad = scaled / root_mean - forward * project_sum / (D * root_mean**3)
    hid_units = down_weight.shape[0]
    gain_grad = lax.psum(gain_part, ("dp", "mp"))
    pieces = lax.all_to_all(out_grad, "dp", split_axis=1, concat_axis=0, tiled=True)
    weight_local = down_weight.astype(jnp.float32)
    partial_value = jnp.dot(
        lax.all_gather(pieces, "mp", axis=0, tiled=True),
        weight_local.T,
        precision=lax.Precision.HIGHEST,
    )
    dp_count = lax.axis_size("dp")
    mp_count = lax.axis_size("mp")
    row_count = out_grad.shape[0]
    partial_value = partial_value.reshape(mp_count, dp_count * row_count, hid_units)
    summed = lax.psum_scatter(partial_value, "dp", scatter_dimension=1, tiled=True)
    hidden_grad = summed.reshape(mp_count * row_count, hid_units)
    gate_val = gate_pre.astype(jnp.float32)
    up_val = up_pre.astype(jnp.float32)
    act_val, pull_back = jax.vjp(gelu_tanh, gate_val)
    gate_grad = pull_back(hidden_grad * up_val)[0]
    up_grad = hidden_grad * act_val
    return (gate_grad, up_grad, gain_grad)


def solution(mesh):
    return jax.shard_map(
        local,
        mesh=mesh,
        in_specs=(
            P(("dp", "mp"), None),
            P(("dp", "mp"), None),
            P(),
            P("mp", "dp"),
            P("dp", "mp"),
            P("dp", "mp"),
        ),
        out_specs=(P("dp", "mp"), P("dp", "mp"), P()),
        check_vma=False,
    )
```

profile of v0, /device:TPU:0, one launch (start us, length us, event | category | flops | bytes accessed | tf_op | source)
XLA Modules:
  0.0 187.1 jit_solution(5941770654814540855)
XLA Ops:
  7.2 0.0 all-gather.2.cloned.1.call-start
  7.2 1.1 fusion.12
  8.3 1.3 fusion.11
  9.5 1.1 fusion.10
  10.7 10.5 %all_to_all.19 = f32[16,4,1152]{2,0,1:T(8,128)} all-to-all(f32[16,4,1152]{2,0,1:T(8,128)S(1)} %bitcast.17), channel_id=1, replica_groups=mesh['dp'=4,'mp'=8] {'dp'}, dimensions={1} | all-to-all | bytes 589824 | tf_op jit(solution)/shard_map/all_to_all | solution.py:27
  21.2 0.0 all-gather.2.cloned.1.call-update
  21.2 0.0 reduce-scatter.2.cloned.1.call-start
  21.3 52.6 %all-gather.2.cloned.1.call-done = f32[512,1152]{1,0:T(8,128)} async-done(((f32[64,1152]{1,0:T(8,128)}), f32[512,1152]{1,0:T(8,128)}) %all-gather.2.cloned.1.call-update) | async-done | bytes 2359312 | tf_op jit(solution)/shard_map/all_gather | solution.py:30
  73.9 23.4 %fusion.16 = f32[512,4608]{1,0:T(8,128)} fusion(f32[512,1152]{1,0:T(8,128)} %all-gather.2.cloned.1.call-done, bf16[4608,1152]{1,0:T(8,128)(2,1)} %param.9), kind=kOutput, calls=%fused_computation.31 | convolution fusion | flops 32614907904 | bytes 22413312 | tf_op jit(solution)/shard_map/dot_general | solution.py:29
  97.2 0.0 copy-start
  97.2 0.0 copy-start.1
  97.3 0.0 reduce-scatter.2.cloned.1.call-update
  97.3 40.2 %psum.7 = f32[4608]{0:T(1024)} all-reduce(f32[4608]{0:T(1024)S(1)} %get-tuple-element.3), channel_id=1, replica_groups=mesh['dp'=4,'mp'=8] {'dp','mp'}, use_global_device_ids=true, to_apply=%region_4.0 | all-reduce | flops 4608 | bytes 36864 | tf_op jit(solution)/shard_map/psum | solution.py:26
  137.5 37.0 %reduce-scatter.2.cloned.1.call-done = f32[8,16,4608]{2,1,0:T(8,128)} async-done(((f32[8,64,4608]{2,1,0:T(8,128)}), f32[8,16,4608]{2,1,0:T(8,128)}) %reduce-scatter.2.cloned.1.call-update) | async-done | bytes 2359312 | tf_op jit(solution)/shard_map/reduce_scatter | solution.py:38
  174.5 0.0 copy-done
  174.5 0.0 copy-done.1
  174.5 5.8 %fusion.8 = (f32[128,4608]{1,0:T(8,128)}, f32[128,4608]{1,0:T(8,128)}) fusion(bf16[128,4608]{1,0:T(8,128)(2,1)S(1)} %copy-done, f32[8,16,4608]{2,1,0:T(8,128)} %reduce-scatter.2.cloned.1.call-done, bf16[128,4608]{1,0:T(8,128)(2,1)S(1)} %copy-done.1), kind=kLoop, calls=%fused_computation.13 | loop fusion | flops 14155776 | bytes 9437184 | tf_op jit(solution)/shard_map/mul | solution.py:44
  (2 shorter events, 0.0 us)
Async XLA Ops:
  7.2 66.7 %all-gather.2.cloned.1.call-start = ((), (), s32[]{:S(2)}) async-start(), calls=%async_computation.2 | async-start | bytes 2654208 | tf_op jit(solution)/shard_map/all_gather | solution.py:30
  21.2 153.3 %reduce-scatter.2.cloned.1.call-start = ((), (), s32[]{:S(2)}) async-start(), calls=%async_computation.3 | async-start | bytes 11796480 | tf_op jit(solution)/shard_map/reduce_scatter | solution.py:38
  97.2 77.3 %copy-start = (bf16[128,4608]{1,0:T(8,128)(2,1)S(1)}, bf16[128,4608]{1,0:T(8,128)(2,1)}, u32[]{:S(2)}) copy-start(bf16[128,4608]{1,0:T(8,128)(2,1)} %param.10) | copy-start | bytes 3538948
  97.2 77.3 %copy-start.1 = (bf16[128,4608]{1,0:T(8,128)(2,1)S(1)}, bf16[128,4608]{1,0:T(8,128)(2,1)}, u32[]{:S(2)}) copy-start(bf16[128,4608]{1,0:T(8,128)(2,1)} %param.11) | copy-start | bytes 3538948
Sparse Core Ops, SparseCore 0:
  21.3 52.5 all-gather.1
  97.4 77.0 reduce-scatter.1
where the time goes:
time: 187 us
  waiting for transfers between devices  89.7 us (48%)
  blocking collectives  50.7 us (27%)
  matrix products  23.4 us (13%)
  between operations  14.1 us (8%)
  other arithmetic  9.22 us (5%)
    all_gather x1, waiting for transfers between devices, local(): lax.all_gather(pieces, 'mp', axis=0, tiled=True)  52.6 us
    psum x1, blocking collectives, local(): gain_grad = lax.psum(gain_part, ('dp', 'mp'))  40.2 us
    reduce_scatter x1, waiting for transfers between devices, local(): lax.psum_scatter(partial_value, 'dp', scatter_dimension=1, tiled=True)  37 us
    dot_general x1, matrix products, local(): jnp.dot(lax.all_gather(pieces, 'mp', axis=0, tiled=True), weight_local.T,...  23.4 us
    all_to_all x1, blocking collectives, local(): lax.all_to_all(out_grad, 'dp', split_axis=1, concat_axis=0, tiled=True)  10.5 us
    mul x1, other arithmetic, local(): up_grad = hidden_grad * act_val  5.78 us
  transfers between devices with their start and end apart: 2, of which 2 were waited for; matrix products, arithmetic and copies ran while one was open for 0% of the time, Pallas kernels for 0%

commit v1 on v0

v1 whole, which is shorter than its diff:
```python
import functools
import math

import jax
import jax.numpy as jnp
from jax import lax
from jax.experimental import pallas as pl
from jax.experimental.pallas import tpu as pltpu
from jax.sharding import PartitionSpec as P

MESH = pl.DeviceIdType.MESH
LANES = 128
WEIGHT_MAX = 0.09375

epsilon = 1e-06


def gelu_tanh(values):
    return jax.nn.gelu(values, approximate=True)


def encode(values, gain):
    v = values * gain
    v2 = v * v
    v4 = v2 * v2
    v8 = v4 * v4
    return jnp.where(v < 0, -v8, v8).astype(jnp.bfloat16)


def decode(codes, gain):
    b = codes.astype(jnp.float32)
    size = jnp.abs(b)
    root = jnp.exp(jnp.log(size) * 0.125) * (1.0 / gain)
    root = jnp.where(size > 0, root, 0.0)
    return jnp.where(b < 0, -root, root)


def kernel(
    dp, mp, gain, tile,
    c_ref, y_ref, post_ref, w_hbm, out_hbm, gain_out,
    w_ref, grad, code, lhs, part, other, sent, got, held, gsum, gsend_a, grecv_a, grecv_b, gblock,
    w_sem, a_send, a_recv, ga_send, ga_recv, g_recv, z_send, y_send, gb_send, gb_recv,
    d_send, d_recv, x_send, x_recv, go_send, go_recv, o_sem,
):
    d, m = lax.axis_index("dp"), lax.axis_index("mp")
    nx, nz = dp // 2, mp // 2
    x, core = d // 2, lax.rem(d, 2)
    z, y = m // 2, lax.rem(m, 2)
    rows, full = c_ref.shape
    feat = full // dp
    hid = w_ref.shape[0]

    def remote(src, dst, send, recv, dev):
        return pltpu.make_async_remote_copy(
            src_ref=src, dst_ref=dst, send_sem=send, recv_sem=recv, device_id=dev, device_id_type=MESH
        )

    w_copy = pltpu.make_async_copy(w_hbm, w_ref, w_sem)
    w_copy.start()

    barrier = pltpu.get_barrier_semaphore()
    for j in range(1, dp):
        pl.semaphore_signal(barrier, inc=1, device_id=(lax.rem(d + j, dp), m), device_id_type=MESH)
    for j in range(1, mp):
        pl.semaphore_signal(barrier, inc=1, device_id=(d, lax.rem(m + j, mp)), device_id_type=MESH)

    forward = y_ref[...].astype(jnp.float32)
    upstream = c_ref[...].astype(jnp.float32)
    inv = 1.0 / jnp.sqrt(jnp.mean(forward * forward, axis=1, keepdims=True) + epsilon)
    normed = forward * inv
    gain_part = jnp.sum(upstream * normed, axis=0, keepdims=True)
    scaled = upstream * post_ref[...]
    mean_prod = jnp.sum(scaled * normed, axis=1, keepdims=True) * (1.0 / full)
    out_grad = (scaled - normed * mean_prod) * inv
    top = jnp.max(jnp.abs(out_grad), axis=1, keepdims=True).astype(jnp.bfloat16).astype(jnp.float32)
    top = jnp.where(top > 1e-37, top, 1.0)
    codes = encode(out_grad * (1.0 / top), gain)
    top_wide = jnp.broadcast_to(top, (rows, LANES)).astype(jnp.bfloat16)
    for t in range(dp):
        code[t, :, :feat] = codes[:, t * feat:(t + 1) * feat]
        code[t, :, feat:] = top_wide
        gsend_a[t] = gain_part[:, t * feat:(t + 1) * feat]
    grad[m, d] = code[d]

    pl.semaphore_wait(barrier, dp - 1 + mp - 1)

    def a_copy(j):
        t = lax.rem(d + j, dp)
        return remote(code.at[t], grad.at[m, d], a_send.at[j], a_recv.at[j], (t, m))

    def ga_copy(j):
        t = lax.rem(d + j, dp)
        return remote(gsend_a.at[t], grecv_a.at[j], ga_send.at[j], ga_recv.at[j], (t, m))

    for j in range(1, dp):
        a_copy(j).start()
    for j in range(1, dp):
        ga_copy(j).start()
    for j in range(1, dp):
        a_copy(j).wait_recv()

    def chunk_z(p):
        odd = lax.rem(p, 2)
        off = odd * ((p + 1) // 2) - (1 - odd) * (p // 2)
        return lax.rem(z + off + nz, nz)

    def chunk(k):
        q = lax.rem(k, 2)
        return 2 * chunk_z(k // 2) + lax.rem(y + q, 2)

    def z_copy(p):
        return remote(grad.at[m], grad.at[m], z_send.at[p], g_recv.at[m], (d, 2 * chunk_z(p) + y))

    def y_copy(p):
        mine = 2 * chunk_z(p) + y
        return remote(grad.at[mine], grad.at[mine], y_send.at[p], g_recv.at[mine], (d, 2 * z + 1 - y))

    def g_wait(mc):
        remote(grad.at[mc], grad.at[mc], y_send.at[0], g_recv.at[mc], (d, 2 * z + 1 - y)).wait_recv()

    y_copy(0).start()
    for p in range(1, nz):
        z_copy(p).start()

    for j in range(1, dp):
        ga_copy(j).wait_recv()
    total = gsend_a[d]
    for j in range(1, dp):
        total = total + grecv_a[j]
    gsum[...] = total

    def gb_copy(j):
        return remote(gsum, grecv_b.at[j], gb_send.at[j], gb_recv.at[j], (d, lax.rem(m + j, mp)))

    for j in range(1, mp):
        gb_copy(j).start()

    w_copy.wait()

    def d_copy(k, xo):
        return remote(
            part.at[k, 2 * xo + 1 - core], other.at[k, xo], d_send.at[k, xo], d_recv.at[k, xo], (2 * x + 1 - core, m)
        )

    def x_copy(k, j):
        return remote(
            sent.at[k, j - 1], got.at[k, j - 1], x_send.at[k, j - 1], x_recv.at[k, j - 1],
            (2 * lax.rem(x + j, nx) + core, m),
        )

    def compute(k):
        mc = chunk(k)
        for t in range(dp):
            value = decode(grad[mc, t][:, :feat], gain)
            high = value.astype(jnp.bfloat16)
            lhs[pl.ds(t * rows, rows), :] = high
            lhs[pl.ds((dp + t) * rows, rows), :] = (value - high.astype(jnp.float32)).astype(jnp.bfloat16)

        def one(i, carry):
            cols = pl.ds(pl.multiple_of(i * tile, tile), tile)
            both = lax.dot_general(
                lhs[...], w_ref[cols, :], (((1,), (1,)), ((), ())), preferred_element_type=jnp.float32
            )
            both = both[: dp * rows] + both[dp * rows:]
            for t in range(dp):
                part[k, t, :, cols] = both[t * rows:(t + 1) * rows]
            return carry

        lax.fori_loop(0, hid // tile, one, 0)
        for j in range(1, nx + 1):
            d_copy(k, lax.rem(x + j, nx)).start()

    def reduce(k):
        for j in range(1, nx):
            xo = lax.rem(x + j, nx)
            d_copy(k, xo).wait_recv()

            def one(i, carry):
                cols = pl.ds(pl.multiple_of(i * tile, tile), tile)
                sent[k, j - 1, :, cols] = encode(part[k, 2 * xo + core, :, cols] + other[k, xo, :, cols], gain)
                return carry

            lax.fori_loop(0, hid // tile, one, 0)
            x_copy(k, j).start()

    def step(k, carry):
        q = lax.rem(k, 2)

        @pl.when(q == 1)
        def _():
            g_wait(chunk(k))

        compute(k)

        @pl.when(jnp.logical_and(q == 0, k + 2 < mp))
        def _():
            g_wait(chunk(k + 2))
            y_copy(k // 2 + 1).start()

        @pl.when(k > 0)
        def _():
            reduce(k - 1)

        return carry

    lax.fori_loop(0, mp, step, 0)
    reduce(mp - 1)

    gtotal = gsum[...]
    for j in range(1, mp):
        gb_copy(j).wait_recv()
        gtotal = gtotal + grecv_b[j]
    gblock[...] = gtotal
    gain_out[d] = gtotal

    def go_copy(j):
        return remote(gblock, gain_out.at[d], go_send.at[j], go_recv.at[j], (lax.rem(d + j, dp), m))

    for j in range(1, dp):
        go_copy(j).start()

    def o_copy(k):
        return pltpu.make_async_copy(held.at[k], out_hbm.at[chunk(k)], o_sem.at[k])

    def finish(k, carry):
        mc = chunk(k)
        d_copy(k, x).wait_recv()
        for j in range(1, nx):
            x_copy(k, j).wait_recv()
        size = grad[mc, d][:, feat:].astype(jnp.float32)[:, :1]

        def one(i, inner):
            cols = pl.ds(pl.multiple_of(i * tile, tile), tile)
            value = part[k, d, :, cols] + other[k, x, :, cols]
            for j in range(1, nx):
                value = value + decode(got[k, j - 1, :, cols], gain)
            held[k, :, cols] = value * size
            return inner

        lax.fori_loop(0, hid // tile, one, 0)
        o_copy(k).start()
        return carry

    lax.fori_loop(0, mp, finish, 0)

    for j in range(1, dp):
        go_copy(j).wait()
        a_copy(j).wait_send()
        ga_copy(j).wait_send()
    for j in range(1, mp):
        gb_copy(j).wait_send()
    for p in range(nz):
        y_copy(p).wait_send()
    for p in range(1, nz):
        z_copy(p).wait_send()

    def drain(k, carry):
        for xo in range(nx):
            d_copy(k, xo).wait_send()
        for j in range(1, nx):
            x_copy(k, j).wait_send()
        o_copy(k).wait()
        return carry

    lax.fori_loop(0, mp, drain, 0)


def fused(dp, mp, cotangent, mlp_out, post_gain, down_weight):
    rows, full = cotangent.shape
    hid, feat = down_weight.shape
    nx, nz = dp // 2, mp // 2
    gain = 2.0 ** math.floor(15.8 - math.log2(full * WEIGHT_MAX))
    tile = next(t for t in (512, 256, 128) if hid % t == 0)
    bf, f32 = jnp.bfloat16, jnp.float32
    dma = pltpu.SemaphoreType.DMA
    hidden, gain_grad = pl.pallas_call(
        functools.partial(kernel, dp, mp, gain, tile),
        out_shape=(jax.ShapeDtypeStruct((mp, rows, hid), f32), jax.ShapeDtypeStruct((dp, 1, feat), f32)),
        in_specs=[pl.BlockSpec(memory_space=pltpu.VMEM)] * 3 + [pl.BlockSpec(memory_space=pl.ANY)],
        out_specs=(pl.BlockSpec(memory_space=pl.ANY), pl.BlockSpec(memory_space=pltpu.VMEM)),
        scratch_shapes=[
            pltpu.VMEM((hid, feat), bf),
            pltpu.VMEM((mp, dp, rows, feat + LANES), bf),
            pltpu.VMEM((dp, rows, feat + LANES), bf),
            pltpu.VMEM((2 * dp * rows, feat), bf),
            pltpu.VMEM((mp, dp, rows, hid), f32),
            pltpu.VMEM((mp, nx, rows, hid), f32),
            pltpu.VMEM((mp, nx - 1, rows, hid), bf),
            pltpu.VMEM((mp, nx - 1, rows, hid), bf),
            pltpu.VMEM((mp, rows, hid), f32),
            pltpu.VMEM((1, feat), f32),
            pltpu.VMEM((dp, 1, feat), f32),
            pltpu.VMEM((dp, 1, feat), f32),
            pltpu.VMEM((mp, 1, feat), f32),
            pltpu.VMEM((1, feat), f32),
            dma, dma((dp,)), dma((dp,)), dma((dp,)), dma((dp,)),
            dma((mp,)), dma((nz,)), dma((nz,)), dma((mp,)), dma((mp,)),
            dma((mp, nx)), dma((mp, nx)), dma((mp, nx)), dma((mp, nx)),
            dma((dp,)), dma((dp,)), dma((mp,)),
        ],
        compiler_params=pltpu.CompilerParams(
            collective_id=0, has_side_effects=True, vmem_limit_bytes=48 * 1024 * 1024
        ),
        name="norm_gather_project_reduce",
    )(cotangent, mlp_out, post_gain.reshape(1, full), down_weight)
    return hidden.reshape(mp * rows, hid), gain_grad.reshape(full)


def plain(cotangent, mlp_out, post_gain, down_weight):
    full = cotangent.shape[1]
    forward = mlp_out.astype(jnp.float32)
    upstream = cotangent.astype(jnp.float32)
    root_mean = jnp.sqrt(jnp.mean(forward * forward, axis=1, keepdims=True) + epsilon)
    normed = forward / root_mean
    gain_part = jnp.sum(upstream * normed, axis=0)
    scaled = upstream * post_gain[None, :]
    project_sum = jnp.sum(scaled * forward, axis=1, keepdims=True)
    out_grad = scaled / root_mean - forward * project_sum / (full * root_mean**3)
    hid_units = down_weight.shape[0]
    gain_grad = lax.psum(gain_part, ("dp", "mp"))
    pieces = lax.all_to_all(out_grad, "dp", split_axis=1, concat_axis=0, tiled=True)
    partial_value = jnp.dot(
        lax.all_gather(pieces, "mp", axis=0, tiled=True),
        down_weight.astype(jnp.float32).T,
        precision=lax.Precision.HIGHEST,
    )
    dp_count = lax.axis_size("dp")
    mp_count = lax.axis_size("mp")
    row_count = out_grad.shape[0]
    partial_value = partial_value.reshape(mp_count, dp_count * row_count, hid_units)
    summed = lax.psum_scatter(partial_value, "dp", scatter_dimension=1, tiled=True)
    return summed.reshape(mp_count * row_count, hid_units), gain_grad


def local(dp, mp, cotangent, mlp_out, post_gain, down_weight, gate_pre, up_pre):
    rows = cotangent.shape[0]
    hid, feat = down_weight.shape
    held_bytes = mp * rows * hid * (4 * dp + 4 * dp // 2 + 2 * dp + 4) + 2 * hid * feat
    tiled = rows % 16 == 0 and hid % LANES == 0 and feat % LANES == 0
    paired = dp % 2 == 0 and mp % 2 == 0 and dp > 2
    if tiled and paired and held_bytes < 40 * 1024 * 1024:
        hidden_grad, gain_grad = fused(dp, mp, cotangent, mlp_out, post_gain, down_weight)
    else:
        hidden_grad, gain_grad = plain(cotangent, mlp_out, post_gain, down_weight)
    gate_val = gate_pre.astype(jnp.float32)
    up_val = up_pre.astype(jnp.float32)
    act_val, pull_back = jax.vjp(gelu_tanh, gate_val)
    gate_grad = pull_back(hidden_grad * up_val)[0]
    up_grad = hidden_grad * act_val
    return (gate_grad, up_grad, gain_grad)


def solution(mesh):
    return jax.shard_map(
        functools.partial(local, mesh.shape["dp"], mesh.shape["mp"]),
        mesh=mesh,
        in_specs=(
            P(("dp", "mp"), None),
            P(("dp", "mp"), None),
            P(),
            P("mp", "dp"),
            P("dp", "mp"),
            P("dp", "mp"),
        ),
        out_specs=(P("dp", "mp"), P("dp", "mp"), P()),
        check_vma=False,
    )
```

time: 187 us -> 71.3 us (0.38)
  waiting for transfers between devices: 89.7 us -> 0 us
  Pallas kernels: 0 us -> 63.1 us
  blocking collectives: 50.7 us -> 0 us
  matrix products: 23.4 us -> 0 us
  between operations: 14.1 us -> 0.67 us
  other arithmetic: 9.22 us -> 4.14 us
  local copies, waits for them, and re-layouts: 0.03 us -> 3.18 us
    pallas_call x0 -> x1, Pallas kernels: none -> 63.1 us  [fused(): pl.pallas_call(functools.partial(kernel, dp, mp, gain, tile), out_shape=(...]
    all_gather x1 -> x0, waiting for transfers between devices: 52.6 us -> none  [local(): lax.all_gather(pieces, 'mp', axis=0, tiled=True)]
    psum x1 -> x0, blocking collectives: 40.2 us -> none  [local(): gain_grad = lax.psum(gain_part, ('dp', 'mp'))]
    reduce_scatter x1 -> x0, waiting for transfers between devices: 37 us -> none  [local(): lax.psum_scatter(partial_value, 'dp', scatter_dimension=1, tiled=True)]
    dot_general x1 -> x0, matrix products: 23.4 us -> none  [local(): jnp.dot(lax.all_gather(pieces, 'mp', axis=0, tiled=True), weight_local.T,...]
    all_to_all x1 -> x0, blocking collectives: 10.5 us -> none  [local(): lax.all_to_all(out_grad, 'dp', split_axis=1, concat_axis=0, tiled=True)]
    reduce_sum x2 -> x0, other arithmetic: 2.31 us -> none  [the longest x1 1.25 us: local(): gain_part = jnp.sum(upstream * normed, axis=0)]
  transfers between devices with their start and end apart: 2 -> 0, of which waited for: 2 -> 0; matrix products, arithmetic and copies ran while one was open for 0% -> 0% of each run, Pallas kernels for 0% -> 0%
where the time goes in v1:
time: 71.3 us; the launch traced here: 71.1 us
  Pallas kernels  63.1 us (88%)
  other arithmetic  4.14 us (6%)
  local copies, waits for them, and re-layouts  3.18 us (4%)
    pallas_call x1, Pallas kernels, fused(): pl.pallas_call(functools.partial(kernel, dp, mp, gain, tile), out_shape=(...  63.1 us
    mul x1, other arithmetic, local(): up_grad = hidden_grad * act_val  4.08 us
    unnamed x8, local copies, waits for them, and re-layouts  1.82 us

profile of v1, /device:TPU:0, one launch (start us, length us, event | category | flops | bytes accessed | tf_op | source)
XLA Modules:
  0.0 71.1 jit_solution(6122152921463837377)
XLA Ops:
  0.6 0.7 %reshape.15.post_ref = f32[1,4608]{1,0:T(1,128)S(1)} reshape(f32[4608]{0:T(1024)} %param.8) | data formatting | bytes 36864 | tf_op jit(solution)/shard_map/reshape | solution.py:305
  1.4 0.0 copy-start
  1.4 0.9 %copy-done = bf16[16,4608]{1,0:T(8,128)(2,1)S(1)} copy-done((bf16[16,4608]{1,0:T(8,128)(2,1)S(1)}, bf16[16,4608]{1,0:T(8,128)(2,1)}, u32[]{:S(2)}) %copy-start) | copy-done | bytes 147480
  2.3 0.0 copy-start.1
  2.3 0.9 %copy-done.1 = bf16[16,4608]{1,0:T(8,128)(2,1)S(1)} copy-done((bf16[16,4608]{1,0:T(8,128)(2,1)S(1)}, bf16[16,4608]{1,0:T(8,128)(2,1)}, u32[]{:S(2)}) %copy-start.1) | copy-done | bytes 147480
  3.2 0.0 copy-start.2
  3.2 0.0 copy-start.3
  3.2 63.1 %norm_gather_project_reduce.1 = (f32[8,16,4608]{2,1,0:T(8,128)S(1)}, f32[4,1,1152]{2,1,0:T(1,128)S(1)}) custom-call(bf16[16,4608]{1,0:T(8,128)(2,1)S(1)} %copy-done, bf16[16,4608]{1,0:T(8,128)(2,1)S(1)} %copy-done.1, f32[1,4608]{1,0:T(1,128)S(1)} %reshape.15.post_ref, bf16[4608,1152]{1,0:T(8,128)(2,1)} %w_hbm.1), custom_call_target="tpu_custom_call" | custom-call | tf_op jit(solution)/shard_map/norm_gather_project_reduce/pallas_call | solution.py:276
  66.3 0.0 copy-done.2
  66.4 0.0 copy-done.3
  66.4 4.1 %fusion.8 = (f32[128,4608]{1,0:T(8,128)}, f32[128,4608]{1,0:T(8,128)}) fusion(bf16[128,4608]{1,0:T(8,128)(2,1)S(1)} %copy-done.2, f32[8,16,4608]{2,1,0:T(8,128)S(1)} %get-tuple-element.5, bf16[128,4608]{1,0:T(8,128)(2,1)S(1)} %copy-done.3), kind=kLoop, calls=%fused_computation.13 | loop fusion | flops 14155776 | bytes 9437184 | tf_op jit(solution)/shard_map/mul | solution.py:349
  70.4 0.1 reduce
  70.5 0.6 reshape.17
Async XLA Ops:
  1.4 0.9 %copy-start = (bf16[16,4608]{1,0:T(8,128)(2,1)S(1)}, bf16[16,4608]{1,0:T(8,128)(2,1)}, u32[]{:S(2)}) copy-start(bf16[16,4608]{1,0:T(8,128)(2,1)} %c_ref.1) | copy-start | bytes 442372
  2.3 0.9 %copy-start.1 = (bf16[16,4608]{1,0:T(8,128)(2,1)S(1)}, bf16[16,4608]{1,0:T(8,128)(2,1)}, u32[]{:S(2)}) copy-start(bf16[16,4608]{1,0:T(8,128)(2,1)} %y_ref.1) | copy-start | bytes 442372
  3.2 63.1 %copy-start.2 = (bf16[128,4608]{1,0:T(8,128)(2,1)S(1)}, bf16[128,4608]{1,0:T(8,128)(2,1)}, u32[]{:S(2)}) copy-start(bf16[128,4608]{1,0:T(8,128)(2,1)} %param.10) | copy-start | bytes 3538948
  3.2 63.2 %copy-start.3 = (bf16[128,4608]{1,0:T(8,128)(2,1)S(1)}, bf16[128,4608]{1,0:T(8,128)(2,1)}, u32[]{:S(2)}) copy-start(bf16[128,4608]{1,0:T(8,128)(2,1)} %param.11) | copy-start | bytes 3538948

commit v2 on v1

--- a/solution.py
+++ b/solution.py
@@ -37,10 +37,10 @@
 
 def kernel(
     dp, mp, gain, tile,
-    c_ref, y_ref, post_ref, w_hbm, out_hbm, gain_out,
-    w_ref, grad, code, lhs, part, other, sent, got, held, gsum, gsend_a, grecv_a, grecv_b, gblock,
+    c_ref, y_ref, post_ref, w_hbm, out_ref, gain_out,
+    w_ref, grad, code, lhs, part, other, sent, got, gsum, gsend_a, grecv_a, grecv_b, gblock,
     w_sem, a_send, a_recv, ga_send, ga_recv, g_recv, z_send, y_send, gb_send, gb_recv,
-    d_send, d_recv, x_send, x_recv, go_send, go_recv, o_sem,
+    d_send, d_recv, x_send, x_recv, go_send, go_recv,
 ):
     d, m = lax.axis_index("dp"), lax.axis_index("mp")
     nx, nz = dp // 2, mp // 2
@@ -48,7 +48,7 @@
     z, y = m // 2, lax.rem(m, 2)
     rows, full = c_ref.shape
     feat = full // dp
-    hid = w_ref.shape[0]
+    half = w_ref.shape[0] // 2
 
     def remote(src, dst, send, recv, dev):
         return pltpu.make_async_remote_copy(
@@ -148,25 +148,33 @@
             (2 * lax.rem(x + j, nx) + core, m),
         )
 
+    def unpack(p):
+        for q in range(2):
+            mc = chunk(2 * p + q)
+            for t in range(dp):
+                value = decode(grad[mc, t][:, :feat], gain)
+                high = value.astype(jnp.bfloat16)
+                at = (2 * t + q) * rows
+                lhs[at:at + rows, :] = high
+                lhs[2 * dp * rows + at:2 * dp * rows + at + rows, :] = (
+                    value - high.astype(jnp.float32)
+                ).astype(jnp.bfloat16)
+
     def compute(k):
-        mc = chunk(k)
-        for t in range(dp):
-            value = decode(grad[mc, t][:, :feat], gain)
-            high = value.astype(jnp.bfloat16)
-            lhs[pl.ds(t * rows, rows), :] = high
-            lhs[pl.ds((dp + t) * rows, rows), :] = (value - high.astype(jnp.float32)).astype(jnp.bfloat16)
+        first = lax.rem(k, 2) * half
 
         def one(i, carry):
+            units = pl.ds(pl.multiple_of(first + i * tile, tile), tile)
             cols = pl.ds(pl.multiple_of(i * tile, tile), tile)
             both = lax.dot_general(
-                lhs[...], w_ref[cols, :], (((1,), (1,)), ((), ())), preferred_element_type=jnp.float32
+                lhs[...], w_ref[units, :], (((1,), (1,)), ((), ())), preferred_element_type=jnp.float32
             )
-            both = both[: dp * rows] + both[dp * rows:]
+            both = both[: 2 * dp * rows] + both[2 * dp * rows:]
             for t in range(dp):
-                part[k, t, :, cols] = both[t * rows:(t + 1) * rows]
+                part[k, t, :, cols] = both[2 * t * rows:2 * (t + 1) * rows]
             return carry
 
-        lax.fori_loop(0, hid // tile, one, 0)
+        lax.fori_loop(0, half // tile, one, 0)
         for j in range(1, nx + 1):
             d_copy(k, lax.rem(x + j, nx)).start()
 
@@ -174,28 +182,31 @@
         for j in range(1, nx):
             xo = lax.rem(x + j, nx)
             d_copy(k, xo).wait_recv()
-
-            def one(i, carry):
-                cols = pl.ds(pl.multiple_of(i * tile, tile), tile)
-                sent[k, j - 1, :, cols] = encode(part[k, 2 * xo + core, :, cols] + other[k, xo, :, cols], gain)
-                return carry
-
-            lax.fori_loop(0, hid // tile, one, 0)
+            sent[k, j - 1] = encode(part[k, 2 * xo + core] + other[k, xo], gain)
             x_copy(k, j).start()
 
+    def pass_on(p):
+        g_wait(chunk(2 * p))
+        y_copy(p).start()
+
     def step(k, carry):
-        q = lax.rem(k, 2)
-
-        @pl.when(q == 1)
+        p, h = k // 2, lax.rem(k, 2)
+
+        @pl.when(h == 0)
         def _():
-            g_wait(chunk(k))
+            g_wait(chunk(k + 1))
+
+            @pl.when(jnp.logical_and(p > 0, p + 1 < nz))
+            def _():
+                pass_on(p + 1)
+
+            unpack(p)
 
         compute(k)
 
-        @pl.when(jnp.logical_and(q == 0, k + 2 < mp))
+        @pl.when(jnp.logical_and(k == 0, nz > 1))
         def _():
-            g_wait(chunk(k + 2))
-            y_copy(k // 2 + 1).start()
+            pass_on(1)
 
         @pl.when(k > 0)
         def _():
@@ -219,26 +230,19 @@
     for j in range(1, dp):
         go_copy(j).start()
 
-    def o_copy(k):
-        return pltpu.make_async_copy(held.at[k], out_hbm.at[chunk(k)], o_sem.at[k])
-
     def finish(k, carry):
-        mc = chunk(k)
+        p, h = k // 2, lax.rem(k, 2)
         d_copy(k, x).wait_recv()
         for j in range(1, nx):
             x_copy(k, j).wait_recv()
-        size = grad[mc, d][:, feat:].astype(jnp.float32)[:, :1]
-
-        def one(i, inner):
-            cols = pl.ds(pl.multiple_of(i * tile, tile), tile)
-            value = part[k, d, :, cols] + other[k, x, :, cols]
-            for j in range(1, nx):
-                value = value + decode(got[k, j - 1, :, cols], gain)
-            held[k, :, cols] = value * size
-            return inner
-
-        lax.fori_loop(0, hid // tile, one, 0)
-        o_copy(k).start()
+        value = part[k, d] + other[k, x]
+        for j in range(1, nx):
+            value = value + decode(got[k, j - 1], gain)
+        cols = pl.ds(pl.multiple_of(h * half, LANES), half)
+        for q in range(2):
+            mc = chunk(2 * p + q)
+            size = grad[mc, d][:, feat:].astype(jnp.float32)[:, :1]
+            out_ref[mc, :, cols] = value[q * rows:(q + 1) * rows] * size
         return carry
 
     lax.fori_loop(0, mp, finish, 0)
@@ -259,7 +263,6 @@
             d_copy(k, xo).wait_send()
         for j in range(1, nx):
             x_copy(k, j).wait_send()
-        o_copy(k).wait()
         return carry
 
     lax.fori_loop(0, mp, drain, 0)
@@ -270,24 +273,24 @@
     hid, feat = down_weight.shape
     nx, nz = dp // 2, mp // 2
     gain = 2.0 ** math.floor(15.8 - math.log2(full * WEIGHT_MAX))
-    tile = next(t for t in (512, 256, 128) if hid % t == 0)
+    half = hid // 2
+    tile = next(t for t in (768, 512, 256, 128) if half % t == 0)
     bf, f32 = jnp.bfloat16, jnp.float32
     dma = pltpu.SemaphoreType.DMA
     hidden, gain_grad = pl.pallas_call(
         functools.partial(kernel, dp, mp, gain, tile),
         out_shape=(jax.ShapeDtypeStruct((mp, rows, hid), f32), jax.ShapeDtypeStruct((dp, 1, feat), f32)),
         in_specs=[pl.BlockSpec(memory_space=pltpu.VMEM)] * 3 + [pl.BlockSpec(memory_space=pl.ANY)],
-        out_specs=(pl.BlockSpec(memory_space=pl.ANY), pl.BlockSpec(memory_space=pltpu.VMEM)),
+        out_specs=(pl.BlockSpec(memory_space=pltpu.VMEM), pl.BlockSpec(memory_space=pltpu.VMEM)),
         scratch_shapes=[
             pltpu.VMEM((hid, feat), bf),
             pltpu.VMEM((mp, dp, rows, feat + LANES), bf),
             pltpu.VMEM((dp, rows, feat + LANES), bf),
-            pltpu.VMEM((2 * dp * rows, feat), bf),
-            pltpu.VMEM((mp, dp, rows, hid), f32),
-            pltpu.VMEM((mp, nx, rows, hid), f32),
-            pltpu.VMEM((mp, nx - 1, rows, hid), bf),
-            pltpu.VMEM((mp, nx - 1, rows, hid), bf),
-            pltpu.VMEM((mp, rows, hid), f32),
+            pltpu.VMEM((4 * dp * rows, feat), bf),
+            pltpu.VMEM((mp, dp, 2 * rows, half), f32),
+            pltpu.VMEM((mp, nx, 2 * rows, half), f32),
+            pltpu.VMEM((mp, nx - 1, 2 * rows, half), bf),
+            pltpu.VMEM((mp, nx - 1, 2 * rows, half), bf),
             pltpu.VMEM((1, feat), f32),
             pltpu.VMEM((dp, 1, feat), f32),
             pltpu.VMEM((dp, 1, feat), f32),
@@ -296,7 +299,7 @@
             dma, dma((dp,)), dma((dp,)), dma((dp,)), dma((dp,)),
             dma((mp,)), dma((nz,)), dma((nz,)), dma((mp,)), dma((mp,)),
             dma((mp, nx)), dma((mp, nx)), dma((mp, nx)), dma((mp, nx)),
-            dma((dp,)), dma((dp,)), dma((mp,)),
+            dma((dp,)), dma((dp,)),
         ],
         compiler_params=pltpu.CompilerParams(
             collective_id=0, has_side_effects=True, vmem_limit_bytes=48 * 1024 * 1024
@@ -336,7 +339,7 @@
     rows = cotangent.shape[0]
     hid, feat = down_weight.shape
     held_bytes = mp * rows * hid * (4 * dp + 4 * dp // 2 + 2 * dp + 4) + 2 * hid * feat
-    tiled = rows % 16 == 0 and hid % LANES == 0 and feat % LANES == 0
+    tiled = rows % 16 == 0 and hid % (2 * LANES) == 0 and feat % LANES == 0
     paired = dp % 2 == 0 and mp % 2 == 0 and dp > 2
     if tiled and paired and held_bytes < 40 * 1024 * 1024:
         hidden_grad, gain_grad = fused(dp, mp, cotangent, mlp_out, post_gain, down_weight)

time: 71.3 us -> 57.8 us (0.81)
  Pallas kernels: 63.1 us -> 49.6 us
    pallas_call x1, Pallas kernels: 63.1 us -> 49.6 us  [fused(): pl.pallas_call(functools.partial(kernel, dp, mp, gain, tile), out_shape=(...]
where the time goes in v2:
time: 57.8 us; the launch traced here: 57.6 us
  Pallas kernels  49.6 us (86%)
  other arithmetic  4.14 us (7%)
  local copies, waits for them, and re-layouts  3.18 us (6%)
  between operations  0.67 us (1%)
    pallas_call x1, Pallas kernels, fused(): pl.pallas_call(functools.partial(kernel, dp, mp, gain, tile), out_shape=(...  49.6 us
    mul x1, other arithmetic, local(): up_grad = hidden_grad * act_val  4.08 us
    unnamed x8, local copies, waits for them, and re-layouts  1.82 us

profile of v2, /device:TPU:0, one launch (start us, length us, event | category | flops | bytes accessed | tf_op | source)
XLA Modules:
  0.0 57.6 jit_solution(1987905368668647876)
XLA Ops:
  0.6 0.7 %reshape.15.post_ref = f32[1,4608]{1,0:T(1,128)S(1)} reshape(f32[4608]{0:T(1024)} %param.8) | data formatting | bytes 36864 | tf_op jit(solution)/shard_map/reshape | solution.py:308
  1.4 0.0 copy-start
  1.4 0.9 %copy-done = bf16[16,4608]{1,0:T(8,128)(2,1)S(1)} copy-done((bf16[16,4608]{1,0:T(8,128)(2,1)S(1)}, bf16[16,4608]{1,0:T(8,128)(2,1)}, u32[]{:S(2)}) %copy-start) | copy-done | bytes 147480
  2.3 0.0 copy-start.1
  2.3 0.9 %copy-done.1 = bf16[16,4608]{1,0:T(8,128)(2,1)S(1)} copy-done((bf16[16,4608]{1,0:T(8,128)(2,1)S(1)}, bf16[16,4608]{1,0:T(8,128)(2,1)}, u32[]{:S(2)}) %copy-start.1) | copy-done | bytes 147480
  3.2 0.0 copy-start.2
  3.2 0.0 copy-start.3
  3.2 49.6 %norm_gather_project_reduce.1 = (f32[8,16,4608]{2,1,0:T(8,128)S(1)}, f32[4,1,1152]{2,1,0:T(1,128)S(1)}) custom-call(bf16[16,4608]{1,0:T(8,128)(2,1)S(1)} %copy-done, bf16[16,4608]{1,0:T(8,128)(2,1)S(1)} %copy-done.1, f32[1,4608]{1,0:T(1,128)S(1)} %reshape.15.post_ref, bf16[4608,1152]{1,0:T(8,128)(2,1)} %w_hbm.1), custom_call_target="tpu_custom_call" | custom-call | tf_op jit(solution)/shard_map/norm_gather_project_reduce/pallas_call | solution.py:280
  52.8 0.0 copy-done.2
  52.8 0.0 copy-done.3
  52.8 4.1 %fusion.8 = (f32[128,4608]{1,0:T(8,128)}, f32[128,4608]{1,0:T(8,128)}) fusion(bf16[128,4608]{1,0:T(8,128)(2,1)S(1)} %copy-done.2, f32[8,16,4608]{2,1,0:T(8,128)S(1)} %get-tuple-element.5, bf16[128,4608]{1,0:T(8,128)(2,1)S(1)} %copy-done.3), kind=kLoop, calls=%fused_computation.13 | loop fusion | flops 14155776 | bytes 9437184 | tf_op jit(solution)/shard_map/mul | solution.py:352
  56.9 0.1 reduce
  57.0 0.6 %reshape.17 = f32[4608]{0:T(1024)} reshape(f32[4,1152]{1,0:T(4,128)S(1)} %reduce) | data formatting | bytes 36864 | tf_op jit(solution)/shard_map/reshape | solution.py:309
Async XLA Ops:
  1.4 0.9 %copy-start = (bf16[16,4608]{1,0:T(8,128)(2,1)S(1)}, bf16[16,4608]{1,0:T(8,128)(2,1)}, u32[]{:S(2)}) copy-start(bf16[16,4608]{1,0:T(8,128)(2,1)} %c_ref.1) | copy-start | bytes 442372
  2.3 0.9 %copy-start.1 = (bf16[16,4608]{1,0:T(8,128)(2,1)S(1)}, bf16[16,4608]{1,0:T(8,128)(2,1)}, u32[]{:S(2)}) copy-start(bf16[16,4608]{1,0:T(8,128)(2,1)} %y_ref.1) | copy-start | bytes 442372
  3.2 49.6 %copy-start.2 = (bf16[128,4608]{1,0:T(8,128)(2,1)S(1)}, bf16[128,4608]{1,0:T(8,128)(2,1)}, u32[]{:S(2)}) copy-start(bf16[128,4608]{1,0:T(8,128)(2,1)} %param.10) | copy-start | bytes 3538948
  3.2 49.6 %copy-start.3 = (bf16[128,4608]{1,0:T(8,128)(2,1)S(1)}, bf16[128,4608]{1,0:T(8,128)(2,1)}, u32[]{:S(2)}) copy-start(bf16[128,4608]{1,0:T(8,128)(2,1)} %param.11) | copy-start | bytes 3538948

commit v3 on v2

--- a/solution.py
+++ b/solution.py
@@ -37,9 +37,9 @@
 
 def kernel(
     dp, mp, gain, tile,
-    c_ref, y_ref, post_ref, w_hbm, out_ref, gain_out,
-    w_ref, grad, code, lhs, part, other, sent, got, gsum, gsend_a, grecv_a, grecv_b, gblock,
-    w_sem, a_send, a_recv, ga_send, ga_recv, g_recv, z_send, y_send, gb_send, gb_recv,
+    c_hbm, y_hbm, post_ref, w_hbm, out_ref, gain_out,
+    c_ref, y_ref, w_ref, grad, code, lhs, part, other, sent, got, gsum, gsend_a, grecv_a, grecv_b, gblock,
+    c_sem, y_sem, w_sem, a_send, a_recv, ga_send, ga_recv, g_recv, z_send, y_send, gb_send, gb_recv,
     d_send, d_recv, x_send, x_recv, go_send, go_recv,
 ):
     d, m = lax.axis_index("dp"), lax.axis_index("mp")
@@ -55,7 +55,11 @@
             src_ref=src, dst_ref=dst, send_sem=send, recv_sem=recv, device_id=dev, device_id_type=MESH
         )
 
+    c_copy = pltpu.make_async_copy(c_hbm, c_ref, c_sem)
+    y_copy_in = pltpu.make_async_copy(y_hbm, y_ref, y_sem)
     w_copy = pltpu.make_async_copy(w_hbm, w_ref, w_sem)
+    y_copy_in.start()
+    c_copy.start()
     w_copy.start()
 
     barrier = pltpu.get_barrier_semaphore()
@@ -64,6 +68,8 @@
     for j in range(1, mp):
         pl.semaphore_signal(barrier, inc=1, device_id=(d, lax.rem(m + j, mp)), device_id_type=MESH)
 
+    y_copy_in.wait()
+    c_copy.wait()
     forward = y_ref[...].astype(jnp.float32)
     upstream = c_ref[...].astype(jnp.float32)
     inv = 1.0 / jnp.sqrt(jnp.mean(forward * forward, axis=1, keepdims=True) + epsilon)
@@ -208,7 +214,11 @@
         def _():
             pass_on(1)
 
-        @pl.when(k > 0)
+        @pl.when(k == 0)
+        def _():
+            reduce(k)
+
+        @pl.when(k > 1)
         def _():
             reduce(k - 1)
 
@@ -280,9 +290,11 @@
     hidden, gain_grad = pl.pallas_call(
         functools.partial(kernel, dp, mp, gain, tile),
         out_shape=(jax.ShapeDtypeStruct((mp, rows, hid), f32), jax.ShapeDtypeStruct((dp, 1, feat), f32)),
-        in_specs=[pl.BlockSpec(memory_space=pltpu.VMEM)] * 3 + [pl.BlockSpec(memory_space=pl.ANY)],
+        in_specs=[pl.BlockSpec(memory_space=s) for s in (pltpu.HBM, pltpu.HBM, pltpu.VMEM, pltpu.HBM)],
         out_specs=(pl.BlockSpec(memory_space=pltpu.VMEM), pl.BlockSpec(memory_space=pltpu.VMEM)),
         scratch_shapes=[
+            pltpu.VMEM((rows, full), bf),
+            pltpu.VMEM((rows, full), bf),
             pltpu.VMEM((hid, feat), bf),
             pltpu.VMEM((mp, dp, rows, feat + LANES), bf),
             pltpu.VMEM((dp, rows, feat + LANES), bf),
@@ -296,7 +308,7 @@
             pltpu.VMEM((dp, 1, feat), f32),
             pltpu.VMEM((mp, 1, feat), f32),
             pltpu.VMEM((1, feat), f32),
-            dma, dma((dp,)), dma((dp,)), dma((dp,)), dma((dp,)),
+            dma, dma, dma, dma((dp,)), dma((dp,)), dma((dp,)), dma((dp,)),
             dma((mp,)), dma((nz,)), dma((nz,)), dma((mp,)), dma((mp,)),
             dma((mp, nx)), dma((mp, nx)), dma((mp, nx)), dma((mp, nx)),
             dma((dp,)), dma((dp,)),

time: 57.8 us -> 58.2 us (level)
  no operation moved by 1% of the time
where the time goes in v3:
time: 58.2 us; the launch traced here: 58 us
  Pallas kernels  50 us (86%)
  other arithmetic  4.14 us (7%)
  local copies, waits for them, and re-layouts  3.18 us (5%)
  between operations  0.67 us (1%)
    pallas_call x1, Pallas kernels, fused(): pl.pallas_call(functools.partial(kernel, dp, mp, gain, tile), out_shape=(...  50 us
    mul x1, other arithmetic, local(): up_grad = hidden_grad * act_val  4.08 us
    unnamed x8, local copies, waits for them, and re-layouts  1.82 us

profile of v3, /device:TPU:0, one launch (start us, length us, event | category | flops | bytes accessed | tf_op | source)
XLA Modules:
  0.0 58.0 jit_solution(15521732398659509595)
XLA Ops:
  0.6 0.7 %reshape.15.post_ref = f32[1,4608]{1,0:T(1,128)S(1)} reshape(f32[4608]{0:T(1024)} %param.8) | data formatting | bytes 36864 | tf_op jit(solution)/shard_map/reshape | solution.py:320
  1.4 0.0 copy-start
  1.4 0.9 %copy-done = bf16[16,4608]{1,0:T(8,128)(2,1)S(1)} copy-done((bf16[16,4608]{1,0:T(8,128)(2,1)S(1)}, bf16[16,4608]{1,0:T(8,128)(2,1)}, u32[]{:S(2)}) %copy-start) | copy-done | bytes 147480
  2.3 0.0 copy-start.1
  2.3 0.9 %copy-done.1 = bf16[16,4608]{1,0:T(8,128)(2,1)S(1)} copy-done((bf16[16,4608]{1,0:T(8,128)(2,1)S(1)}, bf16[16,4608]{1,0:T(8,128)(2,1)}, u32[]{:S(2)}) %copy-start.1) | copy-done | bytes 147480
  3.2 0.0 copy-start.2
  3.2 0.0 copy-start.3
  3.2 50.0 %norm_gather_project_reduce.1 = (f32[8,16,4608]{2,1,0:T(8,128)S(1)}, f32[4,1,1152]{2,1,0:T(1,128)S(1)}) custom-call(bf16[16,4608]{1,0:T(8,128)(2,1)S(1)} %copy-done, bf16[16,4608]{1,0:T(8,128)(2,1)S(1)} %copy-done.1, f32[1,4608]{1,0:T(1,128)S(1)} %reshape.15.post_ref, bf16[4608,1152]{1,0:T(8,128)(2,1)} %w_hbm.1), custom_call_target="tpu_custom_call" | custom-call | tf_op jit(solution)/shard_map/norm_gather_project_reduce/pallas_call | solution.py:290
  53.2 0.0 copy-done.2
  53.2 0.0 copy-done.3
  53.3 4.1 %fusion.8 = (f32[128,4608]{1,0:T(8,128)}, f32[128,4608]{1,0:T(8,128)}) fusion(bf16[128,4608]{1,0:T(8,128)(2,1)S(1)} %copy-done.2, f32[8,16,4608]{2,1,0:T(8,128)S(1)} %get-tuple-element.5, bf16[128,4608]{1,0:T(8,128)(2,1)S(1)} %copy-done.3), kind=kLoop, calls=%fused_computation.13 | loop fusion | flops 14155776 | bytes 9437184 | tf_op jit(solution)/shard_map/mul | solution.py:364
  57.3 0.1 reduce
  57.4 0.6 %reshape.17 = f32[4608]{0:T(1024)} reshape(f32[4,1152]{1,0:T(4,128)S(1)} %reduce) | data formatting | bytes 36864 | tf_op jit(solution)/shard_map/reshape | solution.py:321
Async XLA Ops:
  1.4 0.9 %copy-start = (bf16[16,4608]{1,0:T(8,128)(2,1)S(1)}, bf16[16,4608]{1,0:T(8,128)(2,1)}, u32[]{:S(2)}) copy-start(bf16[16,4608]{1,0:T(8,128)(2,1)} %c_hbm.1) | copy-start | bytes 442372
  2.3 0.9 %copy-start.1 = (bf16[16,4608]{1,0:T(8,128)(2,1)S(1)}, bf16[16,4608]{1,0:T(8,128)(2,1)}, u32[]{:S(2)}) copy-start(bf16[16,4608]{1,0:T(8,128)(2,1)} %y_hbm.1) | copy-start | bytes 442372
  3.2 50.0 %copy-start.2 = (bf16[128,4608]{1,0:T(8,128)(2,1)S(1)}, bf16[128,4608]{1,0:T(8,128)(2,1)}, u32[]{:S(2)}) copy-start(bf16[128,4608]{1,0:T(8,128)(2,1)} %param.10) | copy-start | bytes 3538948
  3.2 50.0 %copy-start.3 = (bf16[128,4608]{1,0:T(8,128)(2,1)S(1)}, bf16[128,4608]{1,0:T(8,128)(2,1)}, u32[]{:S(2)}) copy-start(bf16[128,4608]{1,0:T(8,128)(2,1)} %param.11) | copy-start | bytes 3538948
